TPU v7x, 256 devices: a whole 4x4x8 slice. The times are simulated.
256 devices in a mesh: dp: 16 (over y, x), rows: 16 (over z, core).
Axes of the slice: x: 4, y: 4, z: 8, core: 2. Of those that a mesh axis runs over, the one named last changes fastest.
Arguments:
- grad_out: bfloat16 [8192, 4096], P('dp', 'rows'), may hold values from -0.375 to 0.375
- activations: bfloat16 [8192, 4096], P('dp', 'rows'), may hold values from -6 to 6
- error_feedback: float32 [16, 4096, 4096], P('dp', 'rows'), may hold values from -6 to 6
- momentum: bfloat16 [4096, 4096], P('rows'), may hold values from -1.1953125 to 1.1953125
- right_factor: float32 [4096, 128], P('rows'), may hold values from -0.09375 to 0.09375
Outputs:
- new_error: float32 [16, 4096, 4096], P('dp', 'rows')
- new_momentum: bfloat16 [4096, 4096], P('rows')
- new_right: float32 [4096, 128], P('rows')
All inputs are finite; a program needn't handle non-finite values.
Results may differ from a plain program's by a relative error of at most 0.0012.
Values may be sent and summed in bfloat16 or wider, within the bound.
A program may use at most 64 MiB of HBM per device.

v0:
```python
import jax
import jax.numpy as jnp
from jax import lax
from jax.sharding import PartitionSpec as P

PASSES = 2
MOMENTUM_RATE = 0.9
HIGHEST = lax.Precision.HIGHEST


def from_everyone(value, axis):
    copies = jnp.broadcast_to(value, (lax.axis_size(axis), *value.shape))
    return lax.all_to_all(copies, axis, split_axis=0, concat_axis=0, tiled=True)


def joined_along(tiles, dim):
    lengths = list(tiles.shape[1:])
    lengths[dim] *= tiles.shape[0]
    return jnp.moveaxis(tiles, 0, dim).reshape(lengths)


def gathered_copies(value, axis, dim):
    tiles = from_everyone(value, axis)
    return joined_along(tiles, dim)


def of_everyone(value, axis):
    everything = from_everyone(value, axis)
    return jnp.sum(everything, axis=0)


def total_of_pieces(value, axis):
    return lax.all_gather(value, axis).sum(0)


def cut_along(value, dim, count):
    lengths = value.shape
    tiles = value.reshape(*lengths[:dim], count, lengths[dim] // count, *lengths[dim + 1 :])
    return jnp.moveaxis(tiles, dim, 0)


def sent_and_summed(value, axis, dim):
    count = lax.axis_size(axis)
    tiles = lax.all_to_all(cut_along(value, dim, count), axis, 0, 0, tiled=True)
    return jnp.sum(tiles, axis=0)


def per_device(grad_out, activations, error_feedback, momentum, right_factor):
    replicas = lax.axis_size("dp")
    grad_local = lax.dot_general(
        grad_out,
        lax.all_gather(activations, "rows", axis=1, tiled=True),
        (((0,), (0,)), ((), ())),
        preferred_element_type=jnp.float32,
    )
    merged = grad_local + error_feedback[0]
    right_full = gathered_copies(right_factor, "rows", 0)
    left_factor = None
    own_rows = None
    for pass_index in range(PASSES):
        local_term = jnp.dot(
            merged, right_full, precision=HIGHEST, preferred_element_type=jnp.float32
        )
        left_factor = of_everyone(local_term, "dp") / replicas
        gram_local = jnp.dot(
            left_factor.T, left_factor, precision=HIGHEST, preferred_element_type=jnp.float32
        )
        gram_matrix = total_of_pieces(gram_local, "rows")
        cholesky_lower = jnp.linalg.cholesky(gram_matrix)
        left_factor = jax.scipy.linalg.solve_triangular(cholesky_lower, left_factor.T, lower=True).T
        right_term = lax.dot_general(
            merged,
            left_factor,
            (((0,), (0,)), ((), ())),
            precision=HIGHEST,
            preferred_element_type=jnp.float32,
        )
        own_rows = sent_and_summed(right_term, "rows", 0)
        own_rows = of_everyone(own_rows, "dp") / replicas
        right_full = gathered_copies(own_rows, "rows", 0)
    approx = jnp.dot(
        left_factor, right_full.T, precision=HIGHEST, preferred_element_type=jnp.float32
    )
    new_error = (merged - approx)[None]
    new_momentum = (MOMENTUM_RATE * momentum.astype(jnp.float32) + approx).astype(jnp.bfloat16)
    return (new_error, new_momentum, own_rows)


def solution(mesh):
    return jax.shard_map(
        per_device,
        mesh=mesh,
        in_specs=(
            P("dp", "rows"),
            P("dp", "rows"),
            P("dp", "rows", None),
            P("rows", None),
            P("rows", None),
        ),
        out_specs=(P("dp", "rows", None), P("rows", None), P("rows", None)),
        check_vma=False,
    )
```

profile of v0, /device:TPU:1, one launch (start us, length us, event | category | flops | bytes accessed | tf_op | source)
XLA Modules:
  0.0 616.3 jit_solution(16566047498738973250)
XLA Ops:
  7.2 0.0 copy-start
  7.2 0.0 all-gather.6.cloned.1.call-start
  7.2 0.7 all-gather.6.cloned.1.call-update
  7.9 2.4 broadcast_in_dim.25
  10.3 10.0 %all-to-all-start = ((f32[16,256,128]{2,1,0:T(8,128)}), f32[16,256,128]{2,1,0:T(8,128)S(1)}, u32[]{:S(2)}, u32[]{:S(2)}) async-start(f32[16,256,128]{2,1,0:T(8,128)} %broadcast_in_dim.25), calls=%async_computation | async-start | bytes 4194304 | tf_op jit(solution)/shard_map/all_to_all | solution.py:13
  20.3 0.0 all-gather.8.cloned.1.call-start
  20.4 75.3 %all-gather.6.cloned.1.call-done = bf16[512,4096]{1,0:T(8,128)(2,1)} async-done(((bf16[512,256]{1,0:T(8,128)(2,1)}), bf16[512,4096]{1,0:T(8,128)(2,1)}) %all-gather.6.cloned.1.call-update) | async-done | bytes 4194320 | tf_op jit(solution)/shard_map/all_gather | solution.py:52
  95.7 0.0 copy-done
  95.7 6.8 %convolution_add_fusion = f32[256,4096]{1,0:T(8,128)} fusion(bf16[512,256]{1,0:T(8,128)(2,1)S(1)} %copy-done, bf16[512,4096]{1,0:T(8,128)(2,1)} %all-gather.6.cloned.1.call-done, f32[1,256,4096]{2,1,0:T(8,128)} %param.10), kind=kOutput, calls=%fused_computation | convolution fusion | flops 1074790400 | bytes 12845056 | tf_op jit(solution)/shard_map/dot_general | solution.py:50
  102.5 0.0 all-to-all-done
  102.5 5.9 fusion.26
  108.4 0.2 broadcast_in_dim.26
  108.6 34.5 %all_to_all.45 = f32[16,256,128]{2,1,0:T(8,128)S(1)} all-to-all(f32[16,256,128]{2,1,0:T(8,128)S(1)} %broadcast_in_dim.26), channel_id=1, replica_groups=mesh['dp'=16,'rows'=16] {'dp'}, dimensions={0} | all-to-all | bytes 4194304 | tf_op jit(solution)/shard_map/all_to_all | solution.py:13
  143.1 0.1 reduce_sum.72
  143.2 1.0 fusion.8
  144.2 0.0 all-gather.8.cloned.1.call-update
  144.2 0.2 all-gather.10.cloned.1.call-start
  144.4 34.3 %all-gather.8.cloned.1.call-done = f32[2048,128]{1,0:T(8,128)} async-done(((f32[128,128]{1,0:T(8,128)}), f32[2048,128]{1,0:T(8,128)}) %all-gather.8.cloned.1.call-update) | async-done | bytes 1048592 | tf_op jit(solution)/shard_map/all_gather | solution.py:33
  178.7 1.3 reduce_sum.73
  180.0 0.1 copy.12
  180.1 11.7 %cholesky.44 = f32[128,128]{1,0:T(8,128)S(1)} custom-call(f32[128,128]{1,0:T(8,128)S(1)} %fusion.15), custom_call_target="Cholesky" | custom-call | tf_op jit(solution)/shard_map/jit(cholesky)/cholesky | solution.py:69
  191.9 0.6 compare_reduce_fusion.1
  192.5 0.7 fusion.10
  193.2 9.8 %custom-call.6 = f32[1,128,128]{1,2,0:T(8,128)S(1)} custom-call(f32[1,128,128]{2,1,0:T(8,128)S(1)} %fusion.10), custom_call_target="InvertDiagBlocksLowerTriangular" | custom-call | tf_op jit(solution)/shard_map/jit(_solve_triangular)/triangular_solve | solution.py:70
  203.0 0.3 fusion.2
  203.3 8.7 %fusion.27 = f32[4096,128]{1,0:T(8,128)S(1)} fusion(f32[256,4096]{1,0:T(8,128)} %convolution_add_fusion, f32[128,256]{1,0:T(8,128)S(1)} %fusion.2), kind=kOutput, calls=%fused_computation.41 | convolution fusion | flops 1610612736 | bytes 6422528 | tf_op jit(solution)/shard_map/dot_general | solution.py:71
  212.0 55.3 %all_to_all.46 = f32[16,256,128]{2,1,0:T(8,128)S(1)} all-to-all(f32[16,256,128]{2,1,0:T(8,128)S(1)} %bitcast.49), channel_id=1, replica_groups=mesh['dp'=16,'rows'=16] {'rows'}, dimensions={0} | all-to-all | bytes 4194304 | tf_op jit(solution)/shard_map/all_to_all | solution.py:44
  267.2 0.1 reduce_sum.74
  267.4 0.2 broadcast_in_dim.27
  267.6 34.7 %all_to_all.47 = f32[16,256,128]{2,1,0:T(8,128)S(1)} all-to-all(f32[16,256,128]{2,1,0:T(8,128)S(1)} %broadcast_in_dim.27), channel_id=1, replica_groups=mesh['dp'=16,'rows'=16] {'dp'}, dimensions={0} | all-to-all | bytes 4194304 | tf_op jit(solution)/shard_map/all_to_all | solution.py:13
  302.2 0.1 reduce_sum.75
  302.4 0.2 broadcast_in_dim.28
  302.6 0.0 copy-start.1
  302.6 54.5 %all_to_all.48 = f32[16,256,128]{2,1,0:T(8,128)S(1)} all-to-all(f32[16,256,128]{2,1,0:T(8,128)S(1)} %broadcast_in_dim.28), channel_id=1, replica_groups=mesh['dp'=16,'rows'=16] {'rows'}, dimensions={0} | all-to-all | bytes 4194304 | tf_op jit(solution)/shard_map/all_to_all | solution.py:13
  357.1 0.0 copy-done.1
  357.1 3.5 fusion.28
  360.6 0.2 broadcast_in_dim.29
  360.8 31.1 %all_to_all.49 = f32[16,256,128]{2,1,0:T(8,128)S(1)} all-to-all(f32[16,256,128]{2,1,0:T(8,128)S(1)} %broadcast_in_dim.29), channel_id=1, replica_groups=mesh['dp'=16,'rows'=16] {'dp'}, dimensions={0} | all-to-all | bytes 4194304 | tf_op jit(solution)/shard_map/all_to_all | solution.py:13
  391.9 0.1 reduce_sum.76
  392.0 1.0 fusion.5
  393.0 0.0 all-gather.10.cloned.1.call-update
  393.0 32.6 %all-gather.10.cloned.1.call-done = f32[2048,128]{1,0:T(8,128)} async-done(((f32[128,128]{1,0:T(8,128)}), f32[2048,128]{1,0:T(8,128)}) %all-gather.10.cloned.1.call-update) | async-done | bytes 1048592 | tf_op jit(solution)/shard_map/all_gather | solution.py:33
  425.6 1.3 reduce_sum.77
  426.9 0.1 copy.13
  427.0 11.7 %cholesky.55 = f32[128,128]{1,0:T(8,128)S(1)} custom-call(f32[128,128]{1,0:T(8,128)S(1)} %fusion.13), custom_call_target="Cholesky" | custom-call | tf_op jit(solution)/shard_map/jit(cholesky)/cholesky | solution.py:69
  438.7 0.6 compare_reduce_fusion
  439.4 0.7 fusion.11
  440.1 9.8 %custom-call.7 = f32[1,128,128]{1,2,0:T(8,128)S(1)} custom-call(f32[1,128,128]{2,1,0:T(8,128)S(1)} %fusion.11), custom_call_target="InvertDiagBlocksLowerTriangular" | custom-call | tf_op jit(solution)/shard_map/jit(_solve_triangular)/triangular_solve | solution.py:70
  449.9 0.3 fusion
  450.2 8.7 %fusion.29 = f32[4096,128]{1,0:T(8,128)S(1)} fusion(f32[256,4096]{1,0:T(8,128)} %convolution_add_fusion, f32[128,256]{1,0:T(8,128)S(1)} %fusion), kind=kOutput, calls=%fused_computation.43 | convolution fusion | flops 1610612736 | bytes 6422528 | tf_op jit(solution)/shard_map/dot_general | solution.py:71
  458.8 55.3 %all_to_all.50 = f32[16,256,128]{2,1,0:T(8,128)S(1)} all-to-all(f32[16,256,128]{2,1,0:T(8,128)S(1)} %bitcast.51), channel_id=1, replica_groups=mesh['dp'=16,'rows'=16] {'rows'}, dimensions={0} | all-to-all | bytes 4194304 | tf_op jit(solution)/shard_map/all_to_all | solution.py:44
  514.1 0.1 reduce_sum.78
  514.2 0.2 broadcast_in_dim.30
  514.4 34.7 %all_to_all.51 = f32[16,256,128]{2,1,0:T(8,128)S(1)} all-to-all(f32[16,256,128]{2,1,0:T(8,128)S(1)} %broadcast_in_dim.30), channel_id=1, replica_groups=mesh['dp'=16,'rows'=16] {'dp'}, dimensions={0} | all-to-all | bytes 4194304 | tf_op jit(solution)/shard_map/all_to_all | solution.py:13
  549.1 0.1 reduce_sum.79
  549.2 0.0 copy-start.4
  549.2 0.0 copy-start.3
  549.3 0.2 broadcast_in_dim.31
  549.5 0.0 copy-start.2
  549.5 54.5 %all_to_all.52 = f32[16,256,128]{2,1,0:T(8,128)S(1)} all-to-all(f32[16,256,128]{2,1,0:T(8,128)S(1)} %broadcast_in_dim.31), channel_id=1, replica_groups=mesh['dp'=16,'rows'=16] {'rows'}, dimensions={0} | all-to-all | bytes 4194304 | tf_op jit(solution)/shard_map/all_to_all | solution.py:13
  604.0 0.0 copy-done.4
  604.0 0.0 copy-done.3
  604.0 0.0 copy-done.2
  604.0 5.8 add_convert_fusion
  (6 shorter events, 0.1 us)
Async XLA Ops:
  7.2 88.5 %copy-start = (bf16[512,256]{1,0:T(8,128)(2,1)S(1)}, bf16[512,256]{1,0:T(8,128)(2,1)}, u32[]{:S(2)}) copy-start(bf16[512,256]{1,0:T(8,128)(2,1)} %param.8) | copy-start | bytes 786436
  7.2 88.5 %all-gather.6.cloned.1.call-start = ((), (), s32[]{:S(2)}) async-start(), calls=%async_computation.9 | async-start | bytes 4456448 | tf_op jit(solution)/shard_map/all_gather | solution.py:52
  10.3 92.1 %all-to-all-start = ((f32[16,256,128]{2,1,0:T(8,128)}), f32[16,256,128]{2,1,0:T(8,128)S(1)}, u32[]{:S(2)}, u32[]{:S(2)}) async-start(f32[16,256,128]{2,1,0:T(8,128)} %broadcast_in_dim.25), calls=%async_computation | async-start | bytes 4194304 | tf_op jit(solution)/shard_map/all_to_all | solution.py:13
  20.3 158.4 %all-gather.8.cloned.1.call-start = ((), (), s32[]{:S(2)}) async-start(), calls=%async_computation.10 | async-start | bytes 1114112 | tf_op jit(solution)/shard_map/all_gather | solution.py:33
  144.2 281.4 %all-gather.10.cloned.1.call-start = ((), (), s32[]{:S(2)}) async-start(), calls=%async_computation.11 | async-start | bytes 1114112 | tf_op jit(solution)/shard_map/all_gather | solution.py:33
  302.6 54.6 %copy-start.1 = (f32[256,4096]{1,0:T(8,128)S(1)}, f32[256,4096]{1,0:T(8,128)}, u32[]{:S(2)}) copy-start(f32[256,4096]{1,0:T(8,128)} %convolution_add_fusion) | copy-start | bytes 12582916
  549.2 54.8 %copy-start.4 = (f32[256,128]{1,0:T(8,128)}, f32[256,128]{1,0:T(8,128)S(1)}, u32[]{:S(2)}) copy-start(f32[256,128]{1,0:T(8,128)S(1)} %broadcast_multiply_fusion) | copy-start | bytes 393220
  549.2 54.8 %copy-start.3 = (bf16[256,4096]{1,0:T(8,128)(2,1)S(1)}, bf16[256,4096]{1,0:T(8,128)(2,1)}, u32[]{:S(2)}) copy-start(bf16[256,4096]{1,0:T(8,128)(2,1)} %param.11) | copy-start | bytes 6291460
  549.5 54.6 %copy-start.2 = (f32[256,4096]{1,0:T(8,128)S(1)}, f32[256,4096]{1,0:T(8,128)}, u32[]{:S(2)}) copy-start(f32[256,4096]{1,0:T(8,128)} %convolution_add_fusion) | copy-start | bytes 12582916
Sparse Core Ops, SparseCore 0:
  9.7 85.8 all-gather.5
  144.3 34.3 all-gather.7
  393.1 32.4 all-gather.9
where the time goes:
time: 617 us; the launch traced here: 616 us
  blocking collectives  355 us (58%)
  waiting for transfers between devices  143 us (23%)
  other arithmetic  49 us (8%)
  matrix products  41.9 us (7%)
  between operations  14 us (2%)
  starting transfers between devices  10.3 us (2%)
    all_to_all x6, blocking collectives, from_everyone(): return lax.all_to_all(copies, axis, split_axis=0, concat_axis=0, tiled=True)  244 us
    all_to_all x2, blocking collectives, sent_and_summed(): tiles = lax.all_to_all(cut_along(value, dim, count), axis, 0, 0, tiled=True)  111 us
    all_gather x1, waiting for transfers between devices, per_device(): lax.all_gather(activations, 'rows', axis=1, tiled=True)  75.3 us
    all_gather x2, waiting for transfers between devices, total_of_pieces(): return lax.all_gather(value, axis).sum(0)  66.9 us
    another operation x6, other arithmetic, per_device(): cholesky_lower = jnp.linalg.cholesky(gram_matrix)  24.8 us
    another operation x4, other arithmetic, per_device(): jax.scipy.linalg.solve_triangular(cholesky_lower, left_factor.T, lower=True)  20.9 us
    dot_general x2, matrix products, per_device(): lax.dot_general(merged, left_factor, (((0,), (0,)), ((), ())), precision=...  17.3 us
  transfers between devices with their start and end apart: 4, of which 3 were waited for; matrix products, arithmetic and copies ran while one was open for 1% of the time, Pallas kernels for 0%

commit v1 on v0

--- a/solution.py
+++ b/solution.py
@@ -6,6 +6,11 @@
 PASSES = 2
 MOMENTUM_RATE = 0.9
 HIGHEST = lax.Precision.HIGHEST
+
+
+def tiled_gather(x, axis, dim):
+    copies = jnp.concatenate([x] * lax.axis_size(axis), axis=dim)
+    return lax.all_to_all(copies, axis, dim, dim, tiled=True)
 
 
 def from_everyone(value, axis):
@@ -49,7 +54,7 @@
     replicas = lax.axis_size("dp")
     grad_local = lax.dot_general(
         grad_out,
-        lax.all_gather(activations, "rows", axis=1, tiled=True),
+        tiled_gather(activations, "rows", 1),
         (((0,), (0,)), ((), ())),
         preferred_element_type=jnp.float32,
     )

time: 617 us -> 716 us (1.16)
  blocking collectives: 355 us -> 461 us
  waiting for transfers between devices: 143 us -> 97.1 us
  local copies, waits for them, and re-layouts: 3.81 us -> 36 us
    all_to_all x0 -> x1, blocking collectives: none -> 106 us  [tiled_gather(): return lax.all_to_all(copies, axis, dim, dim, tiled=True)]
    all_gather x1 -> x0, waiting for transfers between devices: 75.3 us -> none  [per_device(): lax.all_gather(activations, 'rows', axis=1, tiled=True)]
    all_to_all x1, waiting for transfers between devices: 0.01 us -> 29.6 us  [from_everyone(): return lax.all_to_all(copies, axis, split_axis=0, concat_axis=0, tiled=True)]
    unnamed x10 -> x32, local copies, waits for them, and re-layouts: 0.03 us -> 14.7 us
    all_to_all x0 -> x2, local copies, waits for them, and re-layouts: none -> 12.8 us  [tiled_gather(): return lax.all_to_all(copies, axis, dim, dim, tiled=True)]
  transfers between devices with their start and end apart: 4 -> 3, of which waited for: 3 -> 3; matrix products, arithmetic and copies ran while one was open for 1% -> 3% of each run, Pallas kernels for 0% -> 0%
where the time goes in v1:
time: 716 us; the launch traced here: 709 us
  blocking collectives  461 us (64%)
  waiting for transfers between devices  97.1 us (14%)
  other arithmetic  55 us (8%)
  matrix products  41 us (6%)
  local copies, waits for them, and re-layouts  36 us (5%)
  between operations  14.6 us (2%)
    all_to_all x6, blocking collectives, from_everyone(): return lax.all_to_all(copies, axis, split_axis=0, concat_axis=0, tiled=True)  244 us
    all_to_all x2, blocking collectives, sent_and_summed(): tiles = lax.all_to_all(cut_along(value, dim, count), axis, 0, 0, tiled=True)  111 us
    all_to_all x1, blocking collectives, tiled_gather(): return lax.all_to_all(copies, axis, dim, dim, tiled=True)  106 us
    all_gather x2, waiting for transfers between devices, total_of_pieces(): return lax.all_gather(value, axis).sum(0)  67.5 us
    all_to_all x1, waiting for transfers between devices, from_everyone(): return lax.all_to_all(copies, axis, split_axis=0, concat_axis=0, tiled=True)  29.6 us
    another operation x6, other arithmetic, per_device(): cholesky_lower = jnp.linalg.cholesky(gram_matrix)  24.8 us
    another operation x4, other arithmetic, per_device(): jax.scipy.linalg.solve_triangular(cholesky_lower, left_factor.T, lower=True)  20.9 us
    dot_general x2, matrix products, per_device(): jnp.dot(merged, right_full, precision=HIGHEST, preferred_element_type=jnp...  15.3 us
  transfers between devices with their start and end apart: 3, of which 3 were waited for; matrix products, arithmetic and copies ran while one was open for 3% of the time, Pallas kernels for 0%

profile of v1, /device:TPU:1, one launch (start us, length us, event | category | flops | bytes accessed | tf_op | source)
XLA Modules:
  0.0 708.7 jit_solution(18333990449300950790)
XLA Ops:
  7.2 0.0 copy-start
  7.2 1.1 copy.41
  8.8 0.0 copy-start.3
  8.8 2.0 copy-done.3
  10.8 6.4 copy.57
  17.2 106.1 %all_to_all.57 = bf16[512,16,256]{2,0,1:T(8,128)(2,1)} all-to-all(bf16[512,16,256]{2,0,1:T(8,128)(2,1)} %copy.57), channel_id=1, replica_groups=mesh['dp'=16,'rows'=16] {'rows'}, dimensions={1} | all-to-all | bytes 8388608 | tf_op jit(solution)/shard_map/all_to_all | solution.py:13
  123.2 1.5 broadcast_in_dim.25
  124.7 3.6 all-to-all-start.1
  128.4 0.0 all-gather.5.cloned.1.call-start
  128.4 5.6 copy.59
  134.0 6.4 copy.58
  140.4 6.7 fusion
  147.1 29.6 %all-to-all-done.1 = f32[16,256,128]{2,1,0:T(8,128)S(1)} async-done(((f32[16,256,128]{2,1,0:T(8,128)}), f32[16,256,128]{2,1,0:T(8,128)S(1)}, u32[]{:S(2)}, u32[]{:S(2)}) %all-to-all-start.1) | async-done | bytes 2097184 | tf_op jit(solution)/shard_map/all_to_all | solution.py:18
  176.7 8.5 %fusion.27 = f32[256,128]{1,0:T(8,128)S(1)} fusion(f32[256,4096]{0,1:T(8,128)} %fusion, f32[4096,128]{1,0:T(8,128)S(1)} %bitcast.54), kind=kOutput, calls=%fused_computation.57 | convolution fusion | flops 1610612736 | bytes 6422528 | tf_op jit(solution)/shard_map/dot_general | solution.py:66
  185.2 0.2 broadcast_in_dim.26
  185.4 34.2 %all_to_all.58 = f32[16,256,128]{2,1,0:T(8,128)S(1)} all-to-all(f32[16,256,128]{2,1,0:T(8,128)S(1)} %broadcast_in_dim.26), channel_id=1, replica_groups=mesh['dp'=16,'rows'=16] {'dp'}, dimensions={0} | all-to-all | bytes 4194304 | tf_op jit(solution)/shard_map/all_to_all | solution.py:18
  219.7 0.1 reduce_sum.72
  219.8 1.0 fusion.9
  220.8 0.0 all-gather.5.cloned.1.call-update
  220.8 0.3 all-gather.7.cloned.1.call-start
  221.2 34.9 %all-gather.5.cloned.1.call-done = f32[2048,128]{1,0:T(8,128)} async-done(((f32[128,128]{1,0:T(8,128)}), f32[2048,128]{1,0:T(8,128)}) %all-gather.5.cloned.1.call-update) | async-done | bytes 1048592 | tf_op jit(solution)/shard_map/all_gather | solution.py:38
  256.0 1.3 reduce_sum.73
  257.3 0.1 copy.60
  257.4 11.7 %cholesky.44 = f32[128,128]{1,0:T(8,128)S(1)} custom-call(f32[128,128]{1,0:T(8,128)S(1)} %fusion.16), custom_call_target="Cholesky" | custom-call | tf_op jit(solution)/shard_map/jit(cholesky)/cholesky | solution.py:74
  269.2 0.6 compare_reduce_fusion.1
  269.8 0.7 fusion.11
  270.5 9.8 %custom-call.6 = f32[1,128,128]{1,2,0:T(8,128)S(1)} custom-call(f32[1,128,128]{2,1,0:T(8,128)S(1)} %fusion.11), custom_call_target="InvertDiagBlocksLowerTriangular" | custom-call | tf_op jit(solution)/shard_map/jit(_solve_triangular)/triangular_solve | solution.py:75
  280.3 0.3 fusion.3
  280.6 5.3 fusion.28
  285.9 55.3 %all_to_all.59 = f32[16,256,128]{2,1,0:T(8,128)S(1)} all-to-all(f32[16,256,128]{2,1,0:T(8,128)S(1)} %bitcast.55), channel_id=1, replica_groups=mesh['dp'=16,'rows'=16] {'rows'}, dimensions={0} | all-to-all | bytes 4194304 | tf_op jit(solution)/shard_map/all_to_all | solution.py:49
  341.2 0.1 reduce_sum.74
  341.3 0.2 broadcast_in_dim.27
  341.5 34.7 %all_to_all.60 = f32[16,256,128]{2,1,0:T(8,128)S(1)} all-to-all(f32[16,256,128]{2,1,0:T(8,128)S(1)} %broadcast_in_dim.27), channel_id=1, replica_groups=mesh['dp'=16,'rows'=16] {'dp'}, dimensions={0} | all-to-all | bytes 4194304 | tf_op jit(solution)/shard_map/all_to_all | solution.py:18
  376.2 0.1 reduce_sum.75
  376.3 0.2 broadcast_in_dim.28
  376.5 55.1 %all_to_all.61 = f32[16,256,128]{2,1,0:T(8,128)S(1)} all-to-all(f32[16,256,128]{2,1,0:T(8,128)S(1)} %broadcast_in_dim.28), channel_id=1, replica_groups=mesh['dp'=16,'rows'=16] {'rows'}, dimensions={0} | all-to-all | bytes 4194304 | tf_op jit(solution)/shard_map/all_to_all | solution.py:18
  431.6 6.8 fusion.29
  438.4 0.2 broadcast_in_dim.29
  438.6 31.2 %all_to_all.62 = f32[16,256,128]{2,1,0:T(8,128)S(1)} all-to-all(f32[16,256,128]{2,1,0:T(8,128)S(1)} %broadcast_in_dim.29), channel_id=1, replica_groups=mesh['dp'=16,'rows'=16] {'dp'}, dimensions={0} | all-to-all | bytes 4194304 | tf_op jit(solution)/shard_map/all_to_all | solution.py:18
  469.8 0.1 reduce_sum.76
  469.9 1.0 fusion.6
  471.0 0.0 all-gather.7.cloned.1.call-update
  471.0 32.6 %all-gather.7.cloned.1.call-done = f32[2048,128]{1,0:T(8,128)} async-done(((f32[128,128]{1,0:T(8,128)}), f32[2048,128]{1,0:T(8,128)}) %all-gather.7.cloned.1.call-update) | async-done | bytes 1048592 | tf_op jit(solution)/shard_map/all_gather | solution.py:38
  503.6 1.3 reduce_sum.77
  504.9 0.1 copy.61
  505.0 11.7 %cholesky.55 = f32[128,128]{1,0:T(8,128)S(1)} custom-call(f32[128,128]{1,0:T(8,128)S(1)} %fusion.14), custom_call_target="Cholesky" | custom-call | tf_op jit(solution)/shard_map/jit(cholesky)/cholesky | solution.py:74
  516.7 0.6 compare_reduce_fusion
  517.4 0.7 fusion.12
  518.0 9.8 %custom-call.7 = f32[1,128,128]{1,2,0:T(8,128)S(1)} custom-call(f32[1,128,128]{2,1,0:T(8,128)S(1)} %fusion.12), custom_call_target="InvertDiagBlocksLowerTriangular" | custom-call | tf_op jit(solution)/shard_map/jit(_solve_triangular)/triangular_solve | solution.py:75
  527.9 0.3 fusion.1
  528.2 5.3 fusion.30
  533.5 55.3 %all_to_all.63 = f32[16,256,128]{2,1,0:T(8,128)S(1)} all-to-all(f32[16,256,128]{2,1,0:T(8,128)S(1)} %bitcast.57), channel_id=1, replica_groups=mesh['dp'=16,'rows'=16] {'rows'}, dimensions={0} | all-to-all | bytes 4194304 | tf_op jit(solution)/shard_map/all_to_all | solution.py:49
  588.7 0.1 reduce_sum.78
  588.9 0.2 broadcast_in_dim.30
  589.1 34.7 %all_to_all.64 = f32[16,256,128]{2,1,0:T(8,128)S(1)} all-to-all(f32[16,256,128]{2,1,0:T(8,128)S(1)} %broadcast_in_dim.30), channel_id=1, replica_groups=mesh['dp'=16,'rows'=16] {'dp'}, dimensions={0} | all-to-all | bytes 4194304 | tf_op jit(solution)/shard_map/all_to_all | solution.py:18
  623.7 0.1 reduce_sum.79
  623.8 0.0 copy-start.4
  623.9 0.0 copy-start.5
  623.9 0.2 broadcast_in_dim.31
  624.1 54.6 %all_to_all.65 = f32[16,256,128]{2,1,0:T(8,128)S(1)} all-to-all(f32[16,256,128]{2,1,0:T(8,128)S(1)} %broadcast_in_dim.31), channel_id=1, replica_groups=mesh['dp'=16,'rows'=16] {'rows'}, dimensions={0} | all-to-all | bytes 4194304 | tf_op jit(solution)/shard_map/all_to_all | solution.py:18
  678.7 5.7 add_convert_fusion
  684.4 5.6 copy.62
  690.0 6.0 subtract_bitcast_fusion
  696.0 5.6 copy.63
  (31 shorter events, 0.4 us)
Async XLA Ops:
  7.2 133.3 %copy-start = (bf16[512,256]{1,0:T(8,128)(2,1)S(1)}, bf16[512,256]{1,0:T(8,128)(2,1)}, u32[]{:S(2)}) copy-start(bf16[512,256]{1,0:T(8,128)(2,1)} %param.8) | copy-start | bytes 786436
  8.8 2.0 copy-start.3
  17.2 106.1 %copy-start.6 = (f32[256,128]{1,0:T(8,128)S(1)}, f32[256,128]{1,0:T(8,128)}, u32[]{:S(2)}) copy-start(f32[256,128]{1,0:T(8,128)} %param.12) | copy-start | bytes 393220
  124.7 52.0 %all-to-all-start.1 = ((f32[16,256,128]{2,1,0:T(8,128)}), f32[16,256,128]{2,1,0:T(8,128)S(1)}, u32[]{:S(2)}, u32[]{:S(2)}) async-start(f32[16,256,128]{2,1,0:T(8,128)} %broadcast_in_dim.25), calls=%async_computation.1 | async-start | bytes 4194304 | tf_op jit(solution)/shard_map/all_to_all | solution.py:18
  128.4 127.7 %all-gather.5.cloned.1.call-start = ((), (), s32[]{:S(2)}) async-start(), calls=%async_computation.10 | async-start | bytes 1114112 | tf_op jit(solution)/shard_map/all_gather | solution.py:38
  220.8 282.7 %all-gather.7.cloned.1.call-start = ((), (), s32[]{:S(2)}) async-start(), calls=%async_computation.11 | async-start | bytes 1114112 | tf_op jit(solution)/shard_map/all_gather | solution.py:38
  376.3 55.3 %copy-start.2 = (f32[256,4096]{0,1:T(8,128)S(1)}, f32[256,4096]{0,1:T(8,128)}, u32[]{:S(2)}) copy-start(f32[256,4096]{0,1:T(8,128)} %fusion) | copy-start | bytes 12582916
  623.8 54.9 %copy-start.4 = (bf16[256,4096]{1,0:T(8,128)(2,1)S(1)}, bf16[256,4096]{1,0:T(8,128)(2,1)}, u32[]{:S(2)}) copy-start(bf16[256,4096]{1,0:T(8,128)(2,1)} %param.11) | copy-start | bytes 6291460
  623.9 60.5 %copy-start.5 = (f32[256,128]{1,0:T(8,128)}, f32[256,128]{1,0:T(8,128)S(1)}, u32[]{:S(2)}) copy-start(f32[256,128]{1,0:T(8,128)S(1)} %broadcast_multiply_fusion) | copy-start | bytes 393220
  690.0 11.6 %copy-start.1 = (bf16[512,256]{1,0:T(8,128)(2,1)S(1)}, bf16[512,256]{1,0:T(8,128)(2,1)}, u32[]{:S(2)}) copy-start(bf16[512,256]{1,0:T(8,128)(2,1)} %param.8) | copy-start | bytes 786436
Sparse Core Ops, SparseCore 0:
  221.0 35.0 all-gather.4
  471.1 32.4 all-gather.6
